TPU v7x, 32 devices: a whole 2x2x4 slice. The times are simulated.
32 devices in a mesh: ka: 8 (over z, x), row: 4 (over y, core).
Axes of the slice: x: 2, y: 2, z: 4, core: 2. Of those that a mesh axis runs over, the one named last changes fastest.
Arguments:
- gauge: bfloat16 [32, 2, 384, 384], P(('ka', 'row')), may hold values from -3 to 3
- energies: float32 [32, 384], P(('ka', 'row')), may hold values from -5 to 5
- kmesh: int32 [3, 32], replicated, may hold values from 0 to 11
- lattice: int32 [3, 256], P(None, 'row'), may hold values from -8 to 8
- degeneracy: int32 [256], P('row'), may hold values from 1 to 8
- path: int32 [3, 8], replicated, may hold values from 0 to 63
Outputs:
- lattice_h: bfloat16 [256, 384, 768], P('row', 'ka')
- path_h: float32 [8, 384, 768], P('row', 'ka')
All inputs are finite; a program needn't handle non-finite values.
Results may differ from a plain program's by a relative error of at most 0.006.
Values may be sent and summed in bfloat16 or wider, within the bound.
No kernel may reach another device: no remote copies, remote signals or barrier semaphores. Data moves between devices by JAX's collectives and lax.ppermute only.
A program may use at most 64 MiB of HBM per device.

v0:
```python
import math
import jax
import jax.numpy as jnp
from jax import lax
from jax.sharding import PartitionSpec as P

MESH = 12
PATH_DEN = 64


def phases(vectors, coords):
    windings = jnp.mod(jnp.sum(vectors[:, :, None] * coords[:, None, :], 0), MESH)
    angles = windings.astype(jnp.float32) * (2.0 * math.pi / MESH)
    return jnp.concatenate([jnp.cos(angles), jnp.sin(angles)], 0).astype(jnp.bfloat16)


def path_factors(path_coords, vectors, counts):
    windings = jnp.mod(jnp.sum(path_coords[:, :, None] * vectors[:, None, :], 0), PATH_DEN)
    angles = windings.astype(jnp.float32) * (2.0 * math.pi / PATH_DEN)
    weights = 1.0 / counts.astype(jnp.float32)
    return jnp.concatenate(
        [jnp.cos(angles) * weights[None, :], jnp.sin(angles) * weights[None, :]], 0
    ).astype(jnp.bfloat16)


def combine_fourier(products, scale_by):
    real_part = products[0, :, :, 0] + products[1, :, :, 1]
    imag_part = products[0, :, :, 1] - products[1, :, :, 0]
    return jnp.concatenate([real_part, imag_part], -1) / scale_by


def combine_path(products):
    real_part = products[0, :, :, 0] - products[1, :, :, 1]
    imag_part = products[0, :, :, 1] + products[1, :, :, 0]
    return jnp.concatenate([real_part, imag_part], -1)


def local(gauge, energies, kmesh, lattice, degeneracy, path):
    per_device = gauge.shape[0]
    orbitals = gauge.shape[2]
    ka_count = lax.axis_size("ka")
    row_count = lax.axis_size("row")
    k_total = kmesh.shape[1]
    path_dev = path.shape[1] // row_count
    scaled = (energies[:, None, :, None] * gauge.astype(jnp.float32)).astype(jnp.bfloat16)
    stacked = jnp.concatenate([gauge[:, 0], gauge[:, 1]], 1)
    partner = jnp.concatenate(
        [
            jnp.concatenate([scaled[:, 0], scaled[:, 1]], 2),
            jnp.concatenate([scaled[:, 1], -scaled[:, 0]], 2),
        ],
        1,
    )
    rotated = jnp.einsum(
        "kna,knb->kab", stacked, partner, preferred_element_type=jnp.float32
    ).astype(jnp.bfloat16)
    arrived = lax.all_to_all(rotated, "ka", split_axis=1, concat_axis=0, tiled=True)
    local_rows = arrived.shape[1]
    lattice_rows = lattice.shape[1]
    k_order = (
        kmesh.reshape(3, ka_count, row_count, per_device).transpose(0, 2, 1, 3).reshape(3, k_total)
    )
    vectors_all, counts_all = (
        lax.all_gather(lattice, "row", axis=1, tiled=True),
        lax.all_gather(degeneracy, "row", axis=0, tiled=True),
    )
    total_vectors = vectors_all.shape[1]
    own_path = lax.dynamic_slice_in_dim(path, lax.axis_index("row") * path_dev, path_dev, 1)
    factors_path = path_factors(own_path, vectors_all, counts_all).astype(jnp.float32)
    factors_mesh = phases(vectors_all, k_order).astype(jnp.float32)
    with_cos = jnp.dot(
        factors_path,
        factors_mesh[:total_vectors],
        preferred_element_type=jnp.float32,
        precision=lax.Precision.HIGHEST,
    )
    with_sin = jnp.dot(
        factors_path,
        factors_mesh[total_vectors:],
        preferred_element_type=jnp.float32,
        precision=lax.Precision.HIGHEST,
    )
    mixing_real = (with_cos[:path_dev] + with_sin[path_dev:]) / k_total
    mixing_imag = (with_cos[path_dev:] - with_sin[:path_dev]) / k_total
    mixing = jnp.concatenate([mixing_real, mixing_imag], 0)
    k_piece = lax.all_gather(arrived, "row", axis=0, tiled=True)
    amount = k_piece.shape[0]
    fourier_amount = k_piece.shape[0]
    factors = phases(lattice, k_order)
    fourier_sum = jnp.dot(
        factors, k_piece.reshape(fourier_amount, -1), preferred_element_type=jnp.float32
    )
    path_sum = jnp.dot(
        mixing,
        k_piece.reshape(amount, -1).astype(jnp.float32),
        preferred_element_type=jnp.float32,
        precision=lax.Precision.HIGHEST,
    )
    summed, path_sum = (fourier_sum, path_sum)
    products = summed.reshape(2, lattice_rows, local_rows, 2, orbitals)
    lattice_f = combine_fourier(products, k_total)
    path_h = combine_path(path_sum.reshape(2, path_dev, local_rows, 2, orbitals))
    lattice_h = lattice_f.astype(jnp.bfloat16)
    return (lattice_h, path_h)


def solution(mesh):
    return jax.shard_map(
        local,
        mesh=mesh,
        in_specs=(
            P(("ka", "row"), None, None, None),
            P(("ka", "row"), None),
            P(),
            P(None, "row"),
            P("row"),
            P(),
        ),
        out_specs=(P("row", "ka", None), P("row", "ka", None)),
        check_vma=False,
    )
```

profile of v0, /device:TPU:0, one launch (start us, length us, event | category | flops | bytes accessed | tf_op | source)
XLA Modules:
  0.0 96.4 jit_solution(5764981165644782622)
XLA Ops:
  7.2 0.0 copy-start
  7.2 0.0 all-gather.3.cloned.1.call-start
  7.2 0.7 reduce
  7.9 1.2 %multiply_convert_fusion = bf16[1,2,384,384]{3,2,1,0:T(8,128)(2,1)S(1)} fusion(bf16[1,2,384,384]{3,2,1,0:T(8,128)(2,1)} %param.6, f32[384]{0:T(512)S(1)} %reduce), kind=kLoop, calls=%fused_computation.23 | loop fusion | flops 884736 | bytes 1181184 | tf_op jit(solution)/shard_map/convert_element_type | solution.py:45
  9.2 1.3 %slice_bitcast_fusion.3 = (bf16[1,384,384]{2,1,0:T(8,128)(2,1)S(1)}, bf16[1,384,384]{2,1,0:T(8,128)(2,1)S(1)}, bf16[1,384,384]{2,1,0:T(8,128)(2,1)S(1)}, bf16[1,384,384]{2,1,0:T(8,128)(2,1)S(1)}) fusion(bf16[1,2,384,384]{3,2,1,0:T(8,128)(2,1)S(1)} %multiply_convert_fusion, bf16[1,2,384,384]{3,2,1,0:T(8,128)(2,1)} %param.6), kind=kLoop, calls=%fused_computation.28 | loop fusion | bytes 2359296 | tf_op jit(solution)/shard_map/squeeze | solution.py:49
  10.5 0.7 fusion.10
  11.1 0.9 copy.83
  12.0 0.5 broadcast.30
  12.6 4.4 %reduce.1 = bf16[384,768]{1,0:T(8,128)(2,1)S(1)} reduce(bf16[384,1,768]{2,1,0:T(2,128)(2,1)S(1)} %bitcast.83, bf16[]{:T(256)} %broadcast.30), dimensions={1}, to_apply=%bitcast.81.reduce_sub_computation | reduce | bytes 1179650
  16.9 0.1 reshape.77
  17.1 23.6 %all_to_all.12 = bf16[8,2,18432]{2,1,0:T(2,128)(2,1)S(1)} all-to-all(bf16[8,2,18432]{2,1,0:T(2,128)(2,1)S(1)} %reshape.77), channel_id=1, replica_groups=mesh['ka'=8,'row'=4] {'ka'}, dimensions={0} | all-to-all | bytes 1179648 | tf_op jit(solution)/shard_map/all_to_all | solution.py:57
  40.7 0.0 copy-start.1
  40.7 0.0 copy-start.2
  40.7 0.0 copy-start.4
  40.7 0.0 copy-start.3
  40.7 0.6 reshape.78
  41.3 0.9 copy.66
  42.2 0.0 all-gather.3.cloned.1.call-update
  42.2 0.0 copy-done.1
  42.2 5.2 %all-gather = s32[4,64,3]{1,2,0:T(4,128)S(1)} all-gather(s32[1,64,3]{1,2,0:T(4,128)S(1)} %bitcast.92), channel_id=1, replica_groups=mesh['ka'=8,'row'=4] {'row'}, dimensions={0}, use_global_device_ids=true | all-gather | bytes 3840 | tf_op jit(solution)/shard_map/all_gather | solution.py:64
  47.4 0.1 reshape.69
  47.5 0.0 copy-done.2
  47.5 0.1 reshape.61
  47.6 0.1 copy.50
  47.7 0.1 mul.87
  47.8 0.1 multiply_reduce_fusion.1
  47.9 0.1 cosine_convert_fusion.1
  47.9 0.1 pad_maximum_fusion.1
  48.0 0.1 convert_element_type.44
  48.1 0.0 copy-done.4
  48.1 0.6 dynamic-slice
  49.4 0.0 copy-done.3
  49.4 0.2 dynamic-update-slice
  49.6 5.2 %all-reduce = s32[256]{0:T(256)S(1)} all-reduce(s32[256]{0:T(256)S(1)} %dynamic-update-slice), channel_id=1, replica_groups=mesh['ka'=8,'row'=4] {'row'}, use_global_device_ids=true, to_apply=%add | all-reduce | flops 256 | bytes 2048
  54.8 0.0 copy-done
  54.8 0.1 constant_dynamic-slice_fusion
  54.9 0.1 multiply_reduce_fusion
  54.9 0.1 multiply_reduce_fusion.2
  55.0 0.1 multiply_convert_fusion.2
  55.1 0.1 multiply_convert_fusion.1
  55.2 0.3 fusion.28
  55.4 0.3 fusion.27
  55.7 9.2 %all-gather.3.cloned.1.call-done = bf16[32,48,768]{2,1,0:T(8,128)(2,1)} async-done(((bf16[8,48,768]{2,1,0:T(8,128)(2,1)}), bf16[32,48,768]{2,1,0:T(8,128)(2,1)}) %all-gather.3.cloned.1.call-update) | async-done | bytes 2359312 | tf_op jit(solution)/shard_map/all_gather | solution.py:86
  64.9 3.8 %copy.71 = bf16[4,8,48,768]{3,1,2,0:T(8,128)(2,1)} copy(bf16[4,8,48,768]{3,2,1,0:T(8,128)(2,1)} %bitcast.86) | data formatting | bytes 4718592
  68.8 3.5 %dot_general.23 = bf16[48,2,384,32]{2,1,0,3:T(2,128)(2,1)S(1)} reshape(bf16[36864,32]{0,1:T(8,128)(2,1)} %bitcast.82) | data formatting | bytes 4718592 | tf_op jit(solution)/shard_map/dot_general | solution.py:90
  72.3 1.5 %fusion.4 = f32[2,2,48,2,384]{4,1,3,2,0:T(2,128)S(1)} fusion(f32[2,2,32,1,1]{2,1,4,3,0:T(2,128)S(1)} %bitcast.91, bf16[48,2,384,32]{2,1,0,3:T(2,128)(2,1)S(1)} %dot_general.23), kind=kOutput, calls=%fused_computation.8 | convolution fusion | flops 56623104 | bytes 2949632 | tf_op jit(solution)/shard_map/dot_general | solution.py:93
  73.8 0.1 fusion.19
  73.9 0.1 fusion.21
  74.0 2.6 %fusion.6 = f32[2,64,48,2,384]{4,1,3,2,0:T(8,128)S(1)} fusion(bf16[48,2,384,32]{2,1,0,3:T(2,128)(2,1)S(1)} %dot_general.23, bf16[2,64,32,1,1]{1,0,2,4,3:T(2,128)(2,1)S(1)} %bitcast.87), kind=kOutput, calls=%fused_computation.10 | convolution fusion | flops 301989888 | bytes 21241856 | tf_op jit(solution)/shard_map/dot_general | solution.py:90
  76.6 0.8 fusion.1
  77.4 0.8 fusion.3
  78.2 0.1 pad_maximum_fusion
  78.3 0.7 copy.61
  79.1 3.3 %fusion = bf16[64,48,768]{2,0,1:T(8,128)(2,1)} fusion(f32[64,48,384]{2,0,1:T(8,128)S(1)} %fusion.1, f32[64,48,384]{2,0,1:T(8,128)S(1)} %fusion.3), kind=kLoop, calls=%fused_computation.1 | loop fusion | flops 7077888 | bytes 14155776 | tf_op jit(solution)/shard_map/convert_element_type | solution.py:103
  82.4 7.1 %copy.60 = bf16[64,48,768]{2,1,0:T(8,128)(2,1)} copy(bf16[64,48,768]{2,0,1:T(8,128)(2,1)} %fusion) | data formatting | bytes 9437184
  (6 shorter events, 0.1 us)
Async XLA Ops:
  7.2 47.6 %copy-start = (s32[3,8]{1,0:T(4,128)S(1)}, s32[3,8]{1,0:T(4,128)}, u32[]{:S(2)}) copy-start(s32[3,8]{1,0:T(4,128)} %param.11) | copy-start | bytes 292
  7.2 57.8 %all-gather.3.cloned.1.call-start = ((), (), s32[]{:S(2)}) async-start(), calls=%async_computation.1 | async-start | bytes 2949120 | tf_op jit(solution)/shard_map/all_gather | solution.py:86
  40.7 1.5 %copy-start.1 = (s32[3,64]{1,0:T(4,128)S(1)}, s32[3,64]{1,0:T(4,128)}, u32[]{:S(2)}) copy-start(s32[3,64]{1,0:T(4,128)} %param.9) | copy-start | bytes 2308
  40.7 6.8 %copy-start.2 = (s32[3,32]{1,0:T(4,128)S(1)}, s32[3,32]{1,0:T(4,128)}, u32[]{:S(2)}) copy-start(s32[3,32]{1,0:T(4,128)} %param.8) | copy-start | bytes 1156
  40.7 7.4 %copy-start.4 = (u32[32]{0:T(128)S(1)}, u32[32]{0:T(128)}, u32[]{:S(2)}) copy-start(u32[32]{0:T(128)} %constant.58) | copy-start | bytes 388
  40.7 8.7 %copy-start.3 = (s32[64]{0:T(128)S(1)}, s32[64]{0:T(128)}, u32[]{:S(2)}) copy-start(s32[64]{0:T(128)} %param.10) | copy-start | bytes 772
Sparse Core Ops, SparseCore 0:
  42.3 22.5 all-gather.2
where the time goes:
time: 96.8 us; the launch traced here: 96.4 us
  blocking collectives  34 us (35%)
  local copies, waits for them, and re-layouts  20.9 us (22%)
  between operations  14.9 us (15%)
  other arithmetic  12 us (12%)
  waiting for transfers between devices  9.25 us (10%)
  matrix products  5.35 us (6%)
    all_to_all x1, blocking collectives, local(): lax.all_to_all(rotated, 'ka', split_axis=1, concat_axis=0, tiled=True)  23.6 us
    unnamed x21, local copies, waits for them, and re-layouts  14.8 us
    all_gather x1, waiting for transfers between devices, local(): k_piece = lax.all_gather(arrived, 'row', axis=0, tiled=True)  9.23 us
    all_gather x1, blocking collectives, local(): lax.all_gather(lattice, 'row', axis=1, tiled=True)  5.19 us
    unnamed x1, blocking collectives  5.15 us
    unnamed x2, other arithmetic  5.07 us
    dot_general x1, local copies, waits for them, and re-layouts, local(): jnp.dot(factors, k_piece.reshape(fourier_amount, -1), preferred_element_t...  3.51 us
    convert_element_type x1, other arithmetic, local(): lattice_h = lattice_f.astype(jnp.bfloat16)  3.29 us
  transfers between devices with their start and end apart: 1, of which 1 were waited for; matrix products, arithmetic and copies ran while one was open for 2% of the time, Pallas kernels for 0%

commit v1 on v0

--- a/solution.py
+++ b/solution.py
@@ -83,7 +83,12 @@
     mixing_real = (with_cos[:path_dev] + with_sin[path_dev:]) / k_total
     mixing_imag = (with_cos[path_dev:] - with_sin[:path_dev]) / k_total
     mixing = jnp.concatenate([mixing_real, mixing_imag], 0)
-    k_piece = lax.all_gather(arrived, "row", axis=0, tiled=True)
+    ring = [arrived]
+    for hop in range(3):
+        ring.append(lax.ppermute(ring[-1], "row", [(dev, (dev + 1) % 4) for dev in range(4)]))
+    k_piece = jnp.roll(
+        jnp.concatenate(ring[::-1], axis=0), (lax.axis_index("row") + 1) * ring[0].shape[0], axis=0
+    )
     amount = k_piece.shape[0]
     fourier_amount = k_piece.shape[0]
     factors = phases(lattice, k_order)

time: 96.8 us -> 88.5 us (0.914)
  blocking collectives: 34 us -> 15 us
  waiting for transfers between devices: 9.25 us -> 26.9 us
  between operations: 14.9 us -> 1.58 us
  starting transfers between devices: 0.04 us -> 7.56 us
  local copies, waits for them, and re-layouts: 20.9 us -> 19.7 us
    all_to_all x1 -> x0, blocking collectives: 23.6 us -> none  [local(): lax.all_to_all(rotated, 'ka', split_axis=1, concat_axis=0, tiled=True)]
    ppermute x0 -> x3, waiting for transfers between devices: none -> 17.5 us  [local(): lax.ppermute(ring[-1], 'row', [(dev, (dev + 1) % 4) for dev in range(4)])]
    all_to_all x0 -> x1, waiting for transfers between devices: none -> 9.44 us  [local(): lax.all_to_all(rotated, 'ka', split_axis=1, concat_axis=0, tiled=True)]
    all_gather x1 -> x0, waiting for transfers between devices: 9.23 us -> none  [local(): k_piece = lax.all_gather(arrived, 'row', axis=0, tiled=True)]
    all_to_all x0 -> x1, starting transfers between devices: none -> 7.28 us  [local(): lax.all_to_all(rotated, 'ka', split_axis=1, concat_axis=0, tiled=True)]
    all_gather x1, blocking collectives: 5.19 us -> 10 us  [local(): lax.all_gather(lattice, 'row', axis=1, tiled=True)]
    unnamed x21 -> x28, local copies, waits for them, and re-layouts: 14.8 us -> 13.4 us
  transfers between devices with their start and end apart: 1 -> 4, of which waited for: 1 -> 3; matrix products, arithmetic and copies ran while one was open for 2% -> 3% of each run, Pallas kernels for 0% -> 0%
where the time goes in v1:
time: 88.5 us; the launch traced here: 88.1 us
  waiting for transfers between devices  26.9 us (30%)
  local copies, waits for them, and re-layouts  19.7 us (22%)
  blocking collectives  15 us (17%)
  other arithmetic  12 us (14%)
  starting transfers between devices  7.56 us (9%)
  matrix products  5.35 us (6%)
  between operations  1.58 us (2%)
    ppermute x3, waiting for transfers between devices, local(): lax.ppermute(ring[-1], 'row', [(dev, (dev + 1) % 4) for dev in range(4)])  17.5 us
    unnamed x28, local copies, waits for them, and re-layouts  13.4 us
    all_gather x1, blocking collectives, local(): lax.all_gather(lattice, 'row', axis=1, tiled=True)  10 us
    all_to_all x1, waiting for transfers between devices, local(): lax.all_to_all(rotated, 'ka', split_axis=1, concat_axis=0, tiled=True)  9.44 us
    all_to_all x1, starting transfers between devices, local(): lax.all_to_all(rotated, 'ka', split_axis=1, concat_axis=0, tiled=True)  7.28 us
    unnamed x2, other arithmetic  5.08 us
    unnamed x1, blocking collectives  4.94 us
    dot_general x1, local copies, waits for them, and re-layouts, local(): jnp.dot(factors, k_piece.reshape(fourier_amount, -1), preferred_element_t...  3.51 us
  transfers between devices with their start and end apart: 4, of which 3 were waited for; matrix products, arithmetic and copies ran while one was open for 3% of the time, Pallas kernels for 0%

profile of v1, /device:TPU:0, one launch (start us, length us, event | category | flops | bytes accessed | tf_op | source)
XLA Modules:
  0.0 88.1 jit_solution(13425541617256375798)
XLA Ops:
  0.6 0.0 copy-start
  0.6 0.7 reduce
  1.3 1.2 %multiply_convert_fusion = bf16[1,2,384,384]{3,2,1,0:T(8,128)(2,1)S(1)} fusion(bf16[1,2,384,384]{3,2,1,0:T(8,128)(2,1)} %param.6, f32[384]{0:T(512)S(1)} %reduce), kind=kLoop, calls=%fused_computation.23 | loop fusion | flops 884736 | bytes 1181184 | tf_op jit(solution)/shard_map/convert_element_type | solution.py:45
  2.6 1.3 %slice_bitcast_fusion.3 = (bf16[1,384,384]{2,1,0:T(8,128)(2,1)S(1)}, bf16[1,384,384]{2,1,0:T(8,128)(2,1)S(1)}, bf16[1,384,384]{2,1,0:T(8,128)(2,1)S(1)}, bf16[1,384,384]{2,1,0:T(8,128)(2,1)S(1)}) fusion(bf16[1,2,384,384]{3,2,1,0:T(8,128)(2,1)S(1)} %multiply_convert_fusion, bf16[1,2,384,384]{3,2,1,0:T(8,128)(2,1)} %param.6), kind=kLoop, calls=%fused_computation.28 | loop fusion | bytes 2359296 | tf_op jit(solution)/shard_map/squeeze | solution.py:49
  3.9 0.0 copy-start.4
  3.9 0.0 copy-start.3
  3.9 0.7 fusion.10
  4.6 0.0 copy-start.1
  4.6 0.0 copy-start.2
  4.6 0.9 %copy.83 = bf16[1,384,768]{2,0,1:T(2,128)(2,1)S(1)} copy(bf16[1,384,768]{2,1,0:T(8,128)(2,1)S(1)} %fusion.10) | data formatting | bytes 1179648 | tf_op jit(solution)/shard_map/convert_element_type | solution.py:56
  5.5 0.5 broadcast.31
  6.0 4.4 %reduce.1 = bf16[384,768]{1,0:T(8,128)(2,1)S(1)} reduce(bf16[384,1,768]{2,1,0:T(2,128)(2,1)S(1)} %bitcast.87, bf16[]{:T(256)} %broadcast.31), dimensions={1}, to_apply=%bitcast.81.reduce_sub_computation | reduce | bytes 1179650
  10.4 1.0 %reshape.77 = bf16[8,2,18432]{2,1,0:T(2,128)(2,1)} reshape(bf16[384,768]{1,0:T(8,128)(2,1)S(1)} %reduce.1) | data formatting | bytes 1179648
  11.4 7.3 %all-to-all-start = ((bf16[8,2,18432]{2,1,0:T(2,128)(2,1)}), bf16[8,2,18432]{2,1,0:T(2,128)(2,1)S(1)}, u32[]{:S(2)}, u32[]{:S(2)}) async-start(bf16[8,2,18432]{2,1,0:T(2,128)(2,1)} %reshape.77), calls=%async_computation | async-start | bytes 1179648 | tf_op jit(solution)/shard_map/all_to_all | solution.py:57
  18.6 0.0 copy-done.4
  18.6 0.6 dynamic-slice
  19.9 0.0 copy-done.3
  19.9 0.2 dynamic-update-slice
  20.1 4.9 %all-reduce = s32[256]{0:T(256)S(1)} all-reduce(s32[256]{0:T(256)S(1)} %dynamic-update-slice), channel_id=1, replica_groups=mesh['ka'=8,'row'=4] {'row'}, use_global_device_ids=true, to_apply=%add | all-reduce | flops 256 | bytes 2048
  25.1 9.4 %all-to-all-done = bf16[8,2,18432]{2,1,0:T(2,128)(2,1)S(1)} async-done(((bf16[8,2,18432]{2,1,0:T(2,128)(2,1)}), bf16[8,2,18432]{2,1,0:T(2,128)(2,1)S(1)}, u32[]{:S(2)}, u32[]{:S(2)}) %all-to-all-start) | async-done | bytes 589856 | tf_op jit(solution)/shard_map/all_to_all | solution.py:57
  34.5 0.6 reshape.78
  35.1 0.1 copy.66
  35.2 0.1 collective-permute-start
  35.3 0.0 copy-done
  35.3 0.1 constant_dynamic-slice_fusion
  35.3 0.0 copy-done.1
  35.3 10.0 %all-gather = s32[4,64,3]{1,2,0:T(4,128)S(1)} all-gather(s32[1,64,3]{1,2,0:T(4,128)S(1)} %bitcast.94), channel_id=1, replica_groups=mesh['ka'=8,'row'=4] {'row'}, dimensions={0}, use_global_device_ids=true | all-gather | bytes 3840 | tf_op jit(solution)/shard_map/all_gather | solution.py:64
  45.4 0.1 reshape.69
  45.5 0.0 copy-done.2
  45.5 0.1 reshape.61
  45.5 0.1 copy.50
  45.6 0.1 mul.90
  45.7 0.1 multiply_reduce_fusion.2
  45.8 0.1 multiply_convert_fusion.2
  45.9 0.1 multiply_convert_fusion.1
  45.9 0.0 collective-permute-done
  45.9 0.2 collective-permute-start.1
  46.2 0.1 multiply_reduce_fusion.1
  46.2 0.1 multiply_reduce_fusion
  46.3 0.1 cosine_convert_fusion.1
  46.4 0.3 fusion.28
  46.7 8.6 %collective-permute-done.1 = bf16[8,48,768]{2,1,0:T(8,128)(2,1)S(1)} collective-permute-done((bf16[8,48,768]{2,1,0:T(8,128)(2,1)S(1)}, bf16[8,48,768]{2,1,0:T(8,128)(2,1)S(1)}, u32[]{:S(2)}, u32[]{:S(2)}) %collective-permute-start.1) | collective-permute-done | bytes 589856 | tf_op jit(solution)/shard_map/ppermute | solution.py:88
  55.3 0.0 collective-permute-start.2
  55.3 0.1 pad_maximum_fusion.1
  55.4 0.1 convert_element_type.44
  55.5 0.3 fusion.27
  55.8 8.9 %collective-permute-done.2 = bf16[8,48,768]{2,1,0:T(8,128)(2,1)S(1)} collective-permute-done((bf16[8,48,768]{2,1,0:T(8,128)(2,1)S(1)}, bf16[8,48,768]{2,1,0:T(8,128)(2,1)S(1)}, u32[]{:S(2)}, u32[]{:S(2)}) %collective-permute-start.2) | collective-permute-done | bytes 589856 | tf_op jit(solution)/shard_map/ppermute | solution.py:88
  65.0 0.2 constant_dynamic-slice_fusion.1
  65.2 2.2 %copy.71 = bf16[4,8,48,768]{3,1,2,0:T(8,128)(2,1)} copy(bf16[4,8,48,768]{3,2,1,0:T(8,128)(2,1)S(1)} %bitcast.82) | data formatting | bytes 4718592
  67.3 3.5 %dot_general.23 = bf16[48,2,384,32]{2,1,0,3:T(2,128)(2,1)S(1)} reshape(bf16[36864,32]{0,1:T(8,128)(2,1)} %bitcast.83) | data formatting | bytes 4718592 | tf_op jit(solution)/shard_map/dot_general | solution.py:95
  70.9 1.5 %fusion.4 = f32[2,2,48,2,384]{4,1,3,2,0:T(2,128)S(1)} fusion(f32[2,2,32,1,1]{2,1,4,3,0:T(2,128)S(1)} %bitcast.93, bf16[48,2,384,32]{2,1,0,3:T(2,128)(2,1)S(1)} %dot_general.23), kind=kOutput, calls=%fused_computation.8 | convolution fusion | flops 56623104 | bytes 2949632 | tf_op jit(solution)/shard_map/dot_general | solution.py:98
  72.4 0.1 fusion.19
  72.5 0.1 fusion.21
  72.6 2.6 %fusion.6 = f32[2,64,48,2,384]{4,1,3,2,0:T(8,128)S(1)} fusion(bf16[48,2,384,32]{2,1,0,3:T(2,128)(2,1)S(1)} %dot_general.23, bf16[2,64,32,1,1]{1,0,2,4,3:T(2,128)(2,1)S(1)} %bitcast.89), kind=kOutput, calls=%fused_computation.10 | convolution fusion | flops 301989888 | bytes 21241856 | tf_op jit(solution)/shard_map/dot_general | solution.py:95
  75.2 0.8 fusion.1
  76.0 0.8 fusion.3
  76.8 0.1 pad_maximum_fusion
  76.9 0.7 copy.61
  77.6 3.3 %fusion = bf16[64,48,768]{2,0,1:T(8,128)(2,1)} fusion(f32[64,48,384]{2,0,1:T(8,128)S(1)} %fusion.1, f32[64,48,384]{2,0,1:T(8,128)S(1)} %fusion.3), kind=kLoop, calls=%fused_computation.1 | loop fusion | flops 7077888 | bytes 14155776 | tf_op jit(solution)/shard_map/convert_element_type | solution.py:108
  80.9 7.1 %copy.60 = bf16[64,48,768]{2,1,0:T(8,128)(2,1)} copy(bf16[64,48,768]{2,0,1:T(8,128)(2,1)} %fusion) | data formatting | bytes 9437184
  (14 shorter events, 0.4 us)
Async XLA Ops:
  0.6 34.6 %copy-start = (s32[3,8]{1,0:T(4,128)S(1)}, s32[3,8]{1,0:T(4,128)}, u32[]{:S(2)}) copy-start(s32[3,8]{1,0:T(4,128)} %param.11) | copy-start | bytes 292
  3.9 14.8 %copy-start.4 = (u32[32]{0:T(128)S(1)}, u32[32]{0:T(128)}, u32[]{:S(2)}) copy-start(u32[32]{0:T(128)} %constant.81) | copy-start | bytes 388
  3.9 16.0 %copy-start.3 = (s32[64]{0:T(128)S(1)}, s32[64]{0:T(128)}, u32[]{:S(2)}) copy-start(s32[64]{0:T(128)} %param.10) | copy-start | bytes 772
  4.6 30.8 %copy-start.1 = (s32[3,64]{1,0:T(4,128)S(1)}, s32[3,64]{1,0:T(4,128)}, u32[]{:S(2)}) copy-start(s32[3,64]{1,0:T(4,128)} %param.9) | copy-start | bytes 2308
  4.6 40.9 %copy-start.2 = (s32[3,32]{1,0:T(4,128)S(1)}, s32[3,32]{1,0:T(4,128)}, u32[]{:S(2)}) copy-start(s32[3,32]{1,0:T(4,128)} %param.8) | copy-start | bytes 1156
  11.4 23.2 %all-to-all-start = ((bf16[8,2,18432]{2,1,0:T(2,128)(2,1)}), bf16[8,2,18432]{2,1,0:T(2,128)(2,1)S(1)}, u32[]{:S(2)}, u32[]{:S(2)}) async-start(bf16[8,2,18432]{2,1,0:T(2,128)(2,1)} %reshape.77), calls=%async_computation | async-start | bytes 1179648 | tf_op jit(solution)/shard_map/all_to_all | solution.py:57
  35.2 10.8 %collective-permute-start = (bf16[8,48,768]{2,1,0:T(8,128)(2,1)S(1)}, bf16[8,48,768]{2,1,0:T(8,128)(2,1)S(1)}, u32[]{:S(2)}, u32[]{:S(2)}) collective-permute-start(bf16[8,48,768]{2,1,0:T(8,128)(2,1)S(1)} %bitcast.84), channel_id=1, source_target_pairs={{0,1},{1,2},{2,3},{3,0},{4,5},{5,6},{6,7},{7,4},{8,9},{9,10},{10,1... | collective-permute-start | bytes 1769480 | tf_op jit(solution)/shard_map/ppermute | solution.py:88
  45.9 9.4 %collective-permute-start.1 = (bf16[8,48,768]{2,1,0:T(8,128)(2,1)S(1)}, bf16[8,48,768]{2,1,0:T(8,128)(2,1)S(1)}, u32[]{:S(2)}, u32[]{:S(2)}) collective-permute-start(bf16[8,48,768]{2,1,0:T(8,128)(2,1)S(1)} %collective-permute-done), channel_id=1, source_target_pairs={{0,1},{1,2},{2,3},{3,0},{4,5},{5,6},{6,7},{7,4},{8,9},{9,10},{10,1... | collective-permute-start | bytes 1769480 | tf_op jit(solution)/shard_map/ppermute | solution.py:88
  55.3 9.3 %collective-permute-start.2 = (bf16[8,48,768]{2,1,0:T(8,128)(2,1)S(1)}, bf16[8,48,768]{2,1,0:T(8,128)(2,1)S(1)}, u32[]{:S(2)}, u32[]{:S(2)}) collective-permute-start(bf16[8,48,768]{2,1,0:T(8,128)(2,1)S(1)} %collective-permute-done.1), channel_id=1, source_target_pairs={{0,1},{1,2},{2,3},{3,0},{4,5},{5,6},{6,7},{7,4},{8,9},{9,10},{10,1... | collective-permute-start | bytes 1769480 | tf_op jit(solution)/shard_map/ppermute | solution.py:88
